TPU v7x, 128 devices: a whole 4x4x4 slice. The times are simulated.
128 devices in a mesh: book: 8 (over y, core), path: 16 (over z, x).
Axes of the slice: x: 4, y: 4, z: 4, core: 2. Of those that a mesh axis runs over, the one named last changes fastest.
Arguments:
- states: float32 [10, 20, 262144], P(None, None, ('book', 'path')), parts along dimension 2, may hold values from -7.5 to 7.5
- itm_flags: int32 [10, 262144], P(None, ('book', 'path')), parts along dimension 1, may hold values 0 or 1
- terminal: float32 [262144], P(('book', 'path')), parts along dimension 0, may hold values from -3.5 to 5.5
- strike: float32 [8], P('book'), parts along dimension 0, may hold values from 0.025 to 0.035
- date_index: int32 [262144], P(('book', 'path')), parts along dimension 0, may hold values from 0 to 9
Outputs:
- cash_flow: float32 [262144], P(('book', 'path')), parts along dimension 0
- book_price: float32 [8], P('book'), parts along dimension 0
- coefficients: float32 [80, 231], P('book'), parts along dimension 0
There are 8 independent parts, one for each index of `book`. A program takes and returns all parts, laid end to end along the dimension named above; each array names one. Nothing has to cross between parts.
All inputs are finite; a program needn't handle non-finite values. No bound on the sum of `itm_flags` on one device may be relied on, other than what follows from the above.
Results may differ from a plain program's by a relative error of at most 0.0003.
Values sent between devices are 32-bit elements; how exact they have to be, the bound alone decides.
A program may use at most 192 MiB of HBM per device.

v0:
```python
import jax
import jax.numpy as jnp
import numpy as np
from jax import lax
from jax.sharding import Mesh
from jax.sharding import PartitionSpec as P

PATH = ("path_0", "path_1")
BOOK_PATH = ("book", "path_0", "path_1")
ridge_weight = 0.05
temper_scale = 0.5
highest = lax.Precision.HIGHEST


def one_axis_at_a_time(shard, axes):
    for axis in axes:
        shard = lax.psum(shard, axis)
    return shard


def sent_to_all(shard, axis):
    length = lax.axis_size(axis)
    return lax.all_to_all(
        jnp.broadcast_to(shard[None], (length, *shard.shape)), axis, 0, 0, tiled=True
    )


def over_copies(shard, axis):
    return sent_to_all(shard, axis).sum(axis=0)


def swap_terms(factors, strike_level):
    forwards = 0.03 * jnp.exp(0.25 * factors)
    discount = jnp.cumprod(1.0 / (1.0 + 0.25 * forwards), axis=0)
    annuity = 0.25 * jnp.sum(discount, axis=0)
    swap_rate = (1.0 - discount[-1]) / annuity
    return (100.0 * annuity * (swap_rate - strike_level), discount[0])


def basis_of(scaled, pair_left, pair_right):
    ones_row = jnp.ones((1, scaled.shape[1]), jnp.float32)
    return jnp.concatenate([ones_row, scaled, scaled[pair_left] * scaled[pair_right]], axis=0)


def gram_only(basis_rows, money_flags):
    weighted = basis_rows * money_flags
    return lax.dot_general(
        weighted,
        basis_rows,
        (((1,), (1,)), ((), ())),
        precision=highest,
        preferred_element_type=jnp.float32,
    )


def system_of(gram_sums, path_count):
    return gram_sums / path_count + ridge_weight * jnp.eye(gram_sums.shape[0], dtype=jnp.float32)


def shards(states, itm_flags, terminal, strike, date_index):
    date_count, factor_count, local_paths = states.shape
    pair_left, pair_right = np.triu_indices(factor_count)
    total_paths = local_paths * lax.axis_size(PATH)
    value_now = terminal
    coef_list = []
    money_all = itm_flags.astype(jnp.float32)
    count_all, first_all, second_all = (
        one_axis_at_a_time(jnp.sum(money_all, axis=1), PATH),
        one_axis_at_a_time(jnp.sum(money_all[:, None, :] * states, axis=2), PATH),
        one_axis_at_a_time(jnp.sum(money_all[:, None, :] * states * states, axis=2), PATH),
    )
    mean_all = first_all / count_all[:, None]
    scale_all = jnp.sqrt(second_all / count_all[:, None] - mean_all * mean_all + 1e-05)
    local_list = []
    for date_step in range(date_count):
        scaled = (states[date_step] - mean_all[date_step][:, None]) / scale_all[date_step][:, None]
        local_list.append(gram_only(basis_of(scaled, pair_left, pair_right), money_all[date_step]))
    gram_stack = lax.psum(jnp.stack(local_list, axis=0), PATH)
    chol_list = [
        jnp.linalg.cholesky(system_of(gram_stack[date_step], count_all[date_step]))
        for date_step in range(date_count)
    ]
    for date_step in range(date_count - 1, -1, -1):
        factors = states[date_step]
        exercise, discount = swap_terms(factors, strike[0])
        value_now = value_now * discount
        money_flags = money_all[date_step]
        scaled = (factors - mean_all[date_step][:, None]) / scale_all[date_step][:, None]
        basis_rows = basis_of(scaled, pair_left, pair_right)
        rhs_local = jnp.dot(
            basis_rows * money_flags,
            value_now,
            precision=highest,
            preferred_element_type=jnp.float32,
        )
        rhs_total = over_copies(rhs_local, PATH)
        coef_vector = jax.scipy.linalg.cho_solve(
            (chol_list[date_step], True), rhs_total / count_all[date_step]
        )
        continuation = jnp.dot(
            coef_vector, basis_rows, precision=highest, preferred_element_type=jnp.float32
        )
        open_date = (date_index <= date_step).astype(jnp.float32)
        weights = jax.nn.sigmoid((exercise - continuation) / temper_scale) * money_flags * open_date
        value_now = value_now + weights * (exercise - value_now)
        coef_list.append(coef_vector)
    book_sum = one_axis_at_a_time(jnp.sum(value_now), PATH)
    book_price = jnp.reshape(book_sum / total_paths, (1,))
    return (value_now, book_price, jnp.stack(coef_list[::-1], axis=0))


def solution(mesh):
    split = Mesh(mesh.devices.reshape(mesh.shape["book"], 4, 4), ("book", "path_0", "path_1"))
    return jax.shard_map(
        shards,
        mesh=split,
        in_specs=(
            P(None, None, BOOK_PATH),
            P(None, BOOK_PATH),
            P(BOOK_PATH),
            P("book"),
            P(BOOK_PATH),
        ),
        out_specs=(P(BOOK_PATH), P("book"), P("book", None)),
        check_vma=False,
    )
```

profile of v0, /device:TPU:0, one launch (start us, length us, event | category | flops | bytes accessed | tf_op | source)
XLA Modules:
  0.0 1114.3 jit_solution(1723377565558352581)
XLA Ops:
  11.3 18.4 %all-reduce.4 = (f32[10,20]{1,0:T(8,128)S(1)}, f32[10]{0:T(128)S(1)}, f32[10,20]{1,0:T(8,128)S(1)}) all-reduce(f32[10,20]{1,0:T(8,128)S(1)} %get-tuple-element.80, f32[10]{0:T(128)S(1)} %convert_reduce_fusion, f32[10,20]{1,0:T(8,128)S(1)} %get-tuple-element.79), channel_id=1, replica_groups=mesh['book'=8,'path_0'=4,'path_1'=4] {'path_0'}, use_global_device_ids=true, to_apply=%region_9.0 | all-reduce | flops 410 | bytes 3280 | tf_op jit(solution)/shard_map/psum | solution.py:17
  29.7 17.0 %all-reduce.3 = (f32[10,20]{1,0:T(8,128)S(1)}, f32[10]{0:T(128)S(1)}, f32[10,20]{1,0:T(8,128)S(1)}) all-reduce(f32[10,20]{1,0:T(8,128)S(1)} %get-tuple-element.84, f32[10]{0:T(128)S(1)} %get-tuple-element.85, f32[10,20]{1,0:T(8,128)S(1)} %get-tuple-element.86), channel_id=1, replica_groups=mesh['book'=8,'path_0'=4,'path_1'=4] {'path_1'}, use_global_device_ids=true, to_apply=%region_10.11 | all-reduce | flops 410 | bytes 3280 | tf_op jit(solution)/shard_map/psum | solution.py:17
  184.8 69.2 %all-reduce.7.cloned.1.call-done = f32[10,231,231]{1,2,0:T(8,128)} async-done(((f32[10,231,231]{1,2,0:T(8,128)}), f32[10,231,231]{1,2,0:T(8,128)}) %all-reduce.7.cloned.1.call-update) | async-done | bytes 2134456 | tf_op jit(solution)/shard_map/psum | solution.py:78
  257.5 11.7 %cholesky.504 = f32[128,128]{1,0:T(8,128)S(1)} custom-call(f32[128,128]{1,0:T(8,128)S(1)} %cholesky.880), custom_call_target="Cholesky" | custom-call | tf_op jit(solution)/shard_map/jit(cholesky)/cholesky | solution.py:80
  304.6 12.1 %cholesky.846 = f32[128,128]{1,0:T(8,128)S(1)} custom-call(f32[128,128]{1,0:T(8,128)S(1)} %cholesky.907), custom_call_target="Cholesky" | custom-call | tf_op jit(solution)/shard_map/jit(cholesky)/cholesky | solution.py:80
  348.6 12.7 %cholesky.808 = f32[128,128]{1,0:T(8,128)S(1)} custom-call(f32[128,128]{1,0:T(8,128)} %cholesky.904), custom_call_target="Cholesky" | custom-call | tf_op jit(solution)/shard_map/jit(cholesky)/cholesky | solution.py:80
  363.2 10.6 custom-call.47
  396.5 12.5 %cholesky.770 = f32[128,128]{1,0:T(8,128)S(1)} custom-call(f32[128,128]{1,0:T(8,128)} %cholesky.901), custom_call_target="Cholesky" | custom-call | tf_op jit(solution)/shard_map/jit(cholesky)/cholesky | solution.py:80
  442.9 11.7 %cholesky.732 = f32[128,128]{1,0:T(8,128)S(1)} custom-call(f32[128,128]{1,0:T(8,128)S(1)} %cholesky.898), custom_call_target="Cholesky" | custom-call | tf_op jit(solution)/shard_map/jit(cholesky)/cholesky | solution.py:80
  484.1 11.7 %cholesky.694 = f32[128,128]{1,0:T(8,128)S(1)} custom-call(f32[128,128]{1,0:T(8,128)S(1)} %cholesky.895), custom_call_target="Cholesky" | custom-call | tf_op jit(solution)/shard_map/jit(cholesky)/cholesky | solution.py:80
  523.6 11.9 %cholesky.656 = f32[128,128]{1,0:T(8,128)S(1)} custom-call(f32[128,128]{1,0:T(8,128)S(1)} %cholesky.892), custom_call_target="Cholesky" | custom-call | tf_op jit(solution)/shard_map/jit(cholesky)/cholesky | solution.py:80
  561.8 11.7 %cholesky.618 = f32[128,128]{1,0:T(8,128)S(1)} custom-call(f32[128,128]{1,0:T(8,128)S(1)} %cholesky.889), custom_call_target="Cholesky" | custom-call | tf_op jit(solution)/shard_map/jit(cholesky)/cholesky | solution.py:80
  600.0 11.7 %cholesky.580 = f32[128,128]{1,0:T(8,128)S(1)} custom-call(f32[128,128]{1,0:T(8,128)S(1)} %cholesky.886), custom_call_target="Cholesky" | custom-call | tf_op jit(solution)/shard_map/jit(cholesky)/cholesky | solution.py:80
  638.1 11.7 %cholesky.542 = f32[128,128]{1,0:T(8,128)S(1)} custom-call(f32[128,128]{1,0:T(8,128)S(1)} %cholesky.883), custom_call_target="Cholesky" | custom-call | tf_op jit(solution)/shard_map/jit(cholesky)/cholesky | solution.py:80
  676.6 19.7 %custom-call.32 = f32[2,128,128]{1,2,0:T(8,128)S(1)} custom-call(f32[2,128,128]{2,1,0:T(8,128)S(1)} %pad_maximum_fusion.10), custom_call_target="InvertDiagBlocksLowerTriangular" | custom-call | tf_op jit(solution)/shard_map/jit(_cho_solve)/triangular_solve | solution.py:97
  719.7 21.1 %custom-call.50 = f32[2,128,128]{1,2,0:T(8,128)} custom-call(f32[2,128,128]{2,1,0:T(8,128)} %pad_maximum_fusion.19), custom_call_target="InvertDiagBlocksLowerTriangular" | custom-call | tf_op jit(solution)/shard_map/jit(_cho_solve)/triangular_solve | solution.py:97
  740.8 21.1 %custom-call.36 = f32[2,128,128]{1,2,0:T(8,128)} custom-call(f32[2,128,128]{2,1,0:T(8,128)} %pad_maximum_fusion.12), custom_call_target="InvertDiagBlocksLowerTriangular" | custom-call | tf_op jit(solution)/shard_map/jit(_cho_solve)/triangular_solve | solution.py:97
  761.9 21.1 %custom-call.38 = f32[2,128,128]{1,2,0:T(8,128)} custom-call(f32[2,128,128]{2,1,0:T(8,128)} %pad_maximum_fusion.13), custom_call_target="InvertDiagBlocksLowerTriangular" | custom-call | tf_op jit(solution)/shard_map/jit(_cho_solve)/triangular_solve | solution.py:97
  783.0 21.1 %custom-call.40 = f32[2,128,128]{1,2,0:T(8,128)} custom-call(f32[2,128,128]{2,1,0:T(8,128)} %pad_maximum_fusion.14), custom_call_target="InvertDiagBlocksLowerTriangular" | custom-call | tf_op jit(solution)/shard_map/jit(_cho_solve)/triangular_solve | solution.py:97
  804.1 21.1 %custom-call.42 = f32[2,128,128]{1,2,0:T(8,128)} custom-call(f32[2,128,128]{2,1,0:T(8,128)} %pad_maximum_fusion.15), custom_call_target="InvertDiagBlocksLowerTriangular" | custom-call | tf_op jit(solution)/shard_map/jit(_cho_solve)/triangular_solve | solution.py:97
  825.2 21.3 %custom-call.44 = f32[2,128,128]{1,2,0:T(8,128)} custom-call(f32[2,128,128]{2,1,0:T(8,128)} %pad_maximum_fusion.16), custom_call_target="InvertDiagBlocksLowerTriangular" | custom-call | tf_op jit(solution)/shard_map/jit(_cho_solve)/triangular_solve | solution.py:97
  846.5 21.1 %custom-call.46 = f32[2,128,128]{1,2,0:T(8,128)} custom-call(f32[2,128,128]{2,1,0:T(8,128)} %pad_maximum_fusion.17), custom_call_target="InvertDiagBlocksLowerTriangular" | custom-call | tf_op jit(solution)/shard_map/jit(_cho_solve)/triangular_solve | solution.py:97
  867.6 21.1 %custom-call.48 = f32[2,128,128]{1,2,0:T(8,128)} custom-call(f32[2,128,128]{2,1,0:T(8,128)} %pad_maximum_fusion.18), custom_call_target="InvertDiagBlocksLowerTriangular" | custom-call | tf_op jit(solution)/shard_map/jit(_cho_solve)/triangular_solve | solution.py:97
  888.7 21.1 %custom-call.34 = f32[2,128,128]{1,2,0:T(8,128)} custom-call(f32[2,128,128]{2,1,0:T(8,128)} %pad_maximum_fusion.11), custom_call_target="InvertDiagBlocksLowerTriangular" | custom-call | tf_op jit(solution)/shard_map/jit(_cho_solve)/triangular_solve | solution.py:97
  (692 shorter events, 637.9 us)
Async XLA Ops:
  9.2 117.4 %copy-start.71 = (f32[1,2048]{1,0:T(1,128)}, f32[1,2048]{1,0:T(1,128)S(1)}, u32[]{:S(2)}) copy-start(f32[1,2048]{1,0:T(1,128)S(1)} %get-tuple-element.145) | copy-start | bytes 24580
  9.2 126.6 %copy-start.75 = (f32[1,2048]{1,0:T(1,128)}, f32[1,2048]{1,0:T(1,128)S(1)}, u32[]{:S(2)}) copy-start(f32[1,2048]{1,0:T(1,128)S(1)} %get-tuple-element.144) | copy-start | bytes 24580
  9.2 129.3 %copy-start.77 = (f32[1,2048]{1,0:T(1,128)}, f32[1,2048]{1,0:T(1,128)S(1)}, u32[]{:S(2)}) copy-start(f32[1,2048]{1,0:T(1,128)S(1)} %get-tuple-element.143) | copy-start | bytes 24580
  9.2 132.0 %copy-start.79 = (f32[1,2048]{1,0:T(1,128)}, f32[1,2048]{1,0:T(1,128)S(1)}, u32[]{:S(2)}) copy-start(f32[1,2048]{1,0:T(1,128)S(1)} %get-tuple-element.142) | copy-start | bytes 24580
  9.3 134.7 %copy-start.81 = (f32[1,2048]{1,0:T(1,128)}, f32[1,2048]{1,0:T(1,128)S(1)}, u32[]{:S(2)}) copy-start(f32[1,2048]{1,0:T(1,128)S(1)} %get-tuple-element.141) | copy-start | bytes 24580
  9.3 137.6 %copy-start.83 = (f32[1,2048]{1,0:T(1,128)}, f32[1,2048]{1,0:T(1,128)S(1)}, u32[]{:S(2)}) copy-start(f32[1,2048]{1,0:T(1,128)S(1)} %get-tuple-element.140) | copy-start | bytes 24580
  9.3 140.3 %copy-start.85 = (f32[1,2048]{1,0:T(1,128)}, f32[1,2048]{1,0:T(1,128)S(1)}, u32[]{:S(2)}) copy-start(f32[1,2048]{1,0:T(1,128)S(1)} %get-tuple-element.139) | copy-start | bytes 24580
  9.3 143.0 %copy-start.88 = (f32[1,2048]{1,0:T(1,128)}, f32[1,2048]{1,0:T(1,128)S(1)}, u32[]{:S(2)}) copy-start(f32[1,2048]{1,0:T(1,128)S(1)} %get-tuple-element.138) | copy-start | bytes 24580
  9.3 145.7 %copy-start.90 = (f32[1,2048]{1,0:T(1,128)}, f32[1,2048]{1,0:T(1,128)S(1)}, u32[]{:S(2)}) copy-start(f32[1,2048]{1,0:T(1,128)S(1)} %get-tuple-element.137) | copy-start | bytes 24580
  9.3 148.4 %copy-start.96 = (f32[1,2048]{1,0:T(1,128)}, f32[1,2048]{1,0:T(1,128)S(1)}, u32[]{:S(2)}) copy-start(f32[1,2048]{1,0:T(1,128)S(1)} %get-tuple-element.146) | copy-start | bytes 24580
  60.6 97.1 %copy-start.127 = (f32[1,2048]{1,0:T(1,128)}, f32[1,2048]{1,0:T(1,128)S(1)}, u32[]{:S(2)}) copy-start(f32[1,2048]{1,0:T(1,128)S(1)} %broadcast.242) | copy-start | bytes 24580
  62.9 121.1 %all-to-all-start = ((f32[16,1,231]{2,1,0:T(1,128)}), f32[16,1,231]{2,1,0:T(1,128)S(1)}, u32[]{:S(2)}, u32[]{:S(2)}) async-start(f32[16,1,231]{2,1,0:T(1,128)} %broadcast_in_dim.208), calls=%async_computation | async-start | bytes 32768 | tf_op jit(solution)/shard_map/all_to_all | solution.py:23
  66.7 187.3 %all-reduce.7.cloned.1.call-start = ((), (), s32[]{:S(2)}) async-start(), calls=%async_computation.10 | async-start | bytes 4751360 | tf_op jit(solution)/shard_map/psum | solution.py:78
  704.3 205.5 %all-to-all-start.1 = ((f32[16,1,231]{2,1,0:T(1,128)}), f32[16,1,231]{2,1,0:T(1,128)}, u32[]{:S(2)}, u32[]{:S(2)}) async-start(f32[16,1,231]{2,1,0:T(1,128)} %broadcast_in_dim.211), calls=%async_computation.1 | async-start | bytes 32768 | tf_op jit(solution)/shard_map/all_to_all | solution.py:23
  713.0 208.9 %copy-start.31 = (f32[210,2048]{1,0:T(8,128)S(1)}, f32[210,2048]{1,0:T(8,128)}, u32[]{:S(2)}) copy-start(f32[210,2048]{1,0:T(8,128)} %copy-done.30) | copy-start | bytes 5160964
  713.0 208.9 %copy-start.89 = (f32[1,2048]{1,0:T(1,128)S(1)}, f32[1,2048]{1,0:T(1,128)}, u32[]{:S(2)}) copy-start(f32[1,2048]{1,0:T(1,128)} %copy-done.88) | copy-start | bytes 24580
  924.3 14.9 %all-to-all-start.2 = ((f32[16,1,231]{2,1,0:T(1,128)}), f32[16,1,231]{2,1,0:T(1,128)S(1)}, u32[]{:S(2)}, u32[]{:S(2)}) async-start(f32[16,1,231]{2,1,0:T(1,128)} %broadcast_in_dim.214), calls=%async_computation.2 | async-start | bytes 32768 | tf_op jit(solution)/shard_map/all_to_all | solution.py:23
  951.0 11.0 all-to-all-start.3
  970.4 11.0 all-to-all-start.4
  990.0 11.4 %all-to-all-start.5 = ((f32[16,1,231]{2,1,0:T(1,128)}), f32[16,1,231]{2,1,0:T(1,128)S(1)}, u32[]{:S(2)}, u32[]{:S(2)}) async-start(f32[16,1,231]{2,1,0:T(1,128)} %broadcast_in_dim.223), calls=%async_computation.5 | async-start | bytes 32768 | tf_op jit(solution)/shard_map/all_to_all | solution.py:23
  1009.8 11.0 all-to-all-start.6
  1029.3 11.0 all-to-all-start.7
  1048.7 11.2 %all-to-all-start.8 = ((f32[16,1,231]{2,1,0:T(1,128)}), f32[16,1,231]{2,1,0:T(1,128)S(1)}, u32[]{:S(2)}, u32[]{:S(2)}) async-start(f32[16,1,231]{2,1,0:T(1,128)} %broadcast_in_dim.232), calls=%async_computation.8 | async-start | bytes 32768 | tf_op jit(solution)/shard_map/all_to_all | solution.py:23
  1068.4 11.0 all-to-all-start.9
  (131 other events, 1780.0 us)
Sparse Core Ops, SparseCore 0:
  160.6 93.2 all-reduce.6
where the time goes:
time: 1120 us; the launch traced here: 1110 us
  other arithmetic  630 us (56%)
  waiting for transfers between devices  127 us (11%)
  matrix products  123 us (11%)
  local copies, waits for them, and re-layouts  106 us (9%)
  blocking collectives  54.3 us (5%)
  starting transfers between devices  41.8 us (4%)
  between operations  31.9 us (3%)
    another operation x70, other arithmetic, shards(): jnp.linalg.cholesky(system_of(gram_stack[date_step], count_all[date_step]))  336 us
    another operation x34, other arithmetic, shards(): jax.scipy.linalg.cho_solve((chol_list[date_step], True), rhs_total / coun...  229 us
    psum x1, waiting for transfers between devices, shards(): gram_stack = lax.psum(jnp.stack(local_list, axis=0), PATH)  69.2 us
    all_to_all x10, waiting for transfers between devices, sent_to_all(): lax.all_to_all(jnp.broadcast_to(shard[None], (length, *shard.shape)), axi...  58 us
    psum x4, blocking collectives, one_axis_at_a_time(): shard = lax.psum(shard, axis)  54.3 us
    all_to_all x10, starting transfers between devices, sent_to_all(): lax.all_to_all(jnp.broadcast_to(shard[None], (length, *shard.shape)), axi...  41.5 us
    another operation x60, matrix products, shards(): jax.scipy.linalg.cho_solve((chol_list[date_step], True), rhs_total / coun...  33.7 us
    dot_general x10, matrix products, gram_only(): lax.dot_general(weighted, basis_rows, (((1,), (1,)), ((), ())), precision...  27.3 us
  transfers between devices with their start and end apart: 11, of which 9 were waited for; matrix products, arithmetic and copies ran while one was open for 27% of the time, Pallas kernels for 0%

commit v1 on v0

--- a/solution.py
+++ b/solution.py
@@ -75,7 +75,7 @@
     for date_step in range(date_count):
         scaled = (states[date_step] - mean_all[date_step][:, None]) / scale_all[date_step][:, None]
         local_list.append(gram_only(basis_of(scaled, pair_left, pair_right), money_all[date_step]))
-    gram_stack = lax.psum(jnp.stack(local_list, axis=0), PATH)
+    gram_stack = lax.psum(lax.psum(jnp.stack(local_list, axis=0), "path_1"), "path_0")
     chol_list = [
         jnp.linalg.cholesky(system_of(gram_stack[date_step], count_all[date_step]))
         for date_step in range(date_count)

time: 1120 us -> 1180 us (1.054)
  waiting for transfers between devices: 127 us -> 167 us
    psum x1 -> x2, waiting for transfers between devices: 69.2 us -> 107 us  [the longest x1 55.6 us: shards(): lax.psum(jnp.stack(local_list, axis=0), 'path_1')]
    dot_general x10, matrix products: 16.6 us -> 28.5 us  [shards(): jnp.dot(basis_rows * money_flags, value_now, precision=highest, preferred...]
    unnamed x288 -> x218, local copies, waits for them, and re-layouts: 22.9 us -> 24.1 us
  transfers between devices with their start and end apart: 11 -> 12, of which waited for: 9 -> 10; matrix products, arithmetic and copies ran while one was open for 27% -> 26% of each run, Pallas kernels for 0% -> 0%
where the time goes in v1:
time: 1180 us; the launch traced here: 1170 us
  other arithmetic  629 us (53%)
  waiting for transfers between devices  167 us (14%)
  matrix products  131 us (11%)
  local copies, waits for them, and re-layouts  109 us (9%)
  blocking collectives  54.3 us (5%)
  starting transfers between devices  42.6 us (4%)
  between operations  31.5 us (3%)
    another operation x70, other arithmetic, shards(): jnp.linalg.cholesky(system_of(gram_stack[date_step], count_all[date_step]))  336 us
    another operation x34, other arithmetic, shards(): jax.scipy.linalg.cho_solve((chol_list[date_step], True), rhs_total / coun...  231 us
    all_to_all x10, waiting for transfers between devices, sent_to_all(): lax.all_to_all(jnp.broadcast_to(shard[None], (length, *shard.shape)), axi...  60.1 us
    psum x1, waiting for transfers between devices, shards(): lax.psum(jnp.stack(local_list, axis=0), 'path_1')  55.6 us
    psum x4, blocking collectives, one_axis_at_a_time(): shard = lax.psum(shard, axis)  54.3 us
    psum x1, waiting for transfers between devices, shards(): lax.psum(lax.psum(jnp.stack(local_list, axis=0), 'path_1'), 'path_0')  51.5 us
    all_to_all x10, starting transfers between devices, sent_to_all(): lax.all_to_all(jnp.broadcast_to(shard[None], (length, *shard.shape)), axi...  42 us
    dot_general x10, matrix products, shards(): jnp.dot(basis_rows * money_flags, value_now, precision=highest, preferred...  28.5 us
  transfers between devices with their start and end apart: 12, of which 10 were waited for; matrix products, arithmetic and copies ran while one was open for 26% of the time, Pallas kernels for 0%

profile of v1, /device:TPU:0, one launch (start us, length us, event | category | flops | bytes accessed | tf_op | source)
XLA Modules:
  0.0 1165.6 jit_solution(16037307403477612320)
XLA Ops:
  11.3 18.4 %all-reduce.4 = (f32[10,20]{1,0:T(8,128)S(1)}, f32[10]{0:T(128)S(1)}, f32[10,20]{1,0:T(8,128)S(1)}) all-reduce(f32[10,20]{1,0:T(8,128)S(1)} %get-tuple-element.80, f32[10]{0:T(128)S(1)} %convert_reduce_fusion, f32[10,20]{1,0:T(8,128)S(1)} %get-tuple-element.79), channel_id=1, replica_groups=mesh['book'=8,'path_0'=4,'path_1'=4] {'path_0'}, use_global_device_ids=true, to_apply=%region_9.0 | all-reduce | flops 410 | bytes 3280 | tf_op jit(solution)/shard_map/psum | solution.py:17
  29.7 17.0 %all-reduce.3 = (f32[10,20]{1,0:T(8,128)S(1)}, f32[10]{0:T(128)S(1)}, f32[10,20]{1,0:T(8,128)S(1)}) all-reduce(f32[10,20]{1,0:T(8,128)S(1)} %get-tuple-element.84, f32[10]{0:T(128)S(1)} %get-tuple-element.85, f32[10,20]{1,0:T(8,128)S(1)} %get-tuple-element.86), channel_id=1, replica_groups=mesh['book'=8,'path_0'=4,'path_1'=4] {'path_1'}, use_global_device_ids=true, to_apply=%region_10.0 | all-reduce | flops 410 | bytes 3280 | tf_op jit(solution)/shard_map/psum | solution.py:17
  170.0 55.6 %all-reduce.8.cloned.1.call-done = f32[10,231,231]{1,2,0:T(8,128)} async-done(((f32[10,231,231]{1,2,0:T(8,128)}), f32[10,231,231]{1,2,0:T(8,128)}) %all-reduce.8.cloned.1.call-update) | async-done | bytes 2134456 | tf_op jit(solution)/shard_map/psum | solution.py:78
  239.9 51.5 %all-reduce.10.cloned.1.call-done = f32[10,231,231]{1,2,0:T(8,128)} async-done(((f32[10,231,231]{1,2,0:T(8,128)}), f32[10,231,231]{1,2,0:T(8,128)}) %all-reduce.10.cloned.1.call-update) | async-done | bytes 2134456 | tf_op jit(solution)/shard_map/psum | solution.py:78
  294.8 11.7 %cholesky.504 = f32[128,128]{1,0:T(8,128)S(1)} custom-call(f32[128,128]{1,0:T(8,128)S(1)} %cholesky.880), custom_call_target="Cholesky" | custom-call | tf_op jit(solution)/shard_map/jit(cholesky)/cholesky | solution.py:80
  342.2 12.1 %cholesky.846 = f32[128,128]{1,0:T(8,128)S(1)} custom-call(f32[128,128]{1,0:T(8,128)S(1)} %cholesky.907), custom_call_target="Cholesky" | custom-call | tf_op jit(solution)/shard_map/jit(cholesky)/cholesky | solution.py:80
  386.1 12.7 %cholesky.808 = f32[128,128]{1,0:T(8,128)S(1)} custom-call(f32[128,128]{1,0:T(8,128)} %cholesky.904), custom_call_target="Cholesky" | custom-call | tf_op jit(solution)/shard_map/jit(cholesky)/cholesky | solution.py:80
  434.0 12.5 %cholesky.770 = f32[128,128]{1,0:T(8,128)S(1)} custom-call(f32[128,128]{1,0:T(8,128)} %cholesky.901), custom_call_target="Cholesky" | custom-call | tf_op jit(solution)/shard_map/jit(cholesky)/cholesky | solution.py:80
  480.3 11.7 %cholesky.732 = f32[128,128]{1,0:T(8,128)S(1)} custom-call(f32[128,128]{1,0:T(8,128)S(1)} %cholesky.898), custom_call_target="Cholesky" | custom-call | tf_op jit(solution)/shard_map/jit(cholesky)/cholesky | solution.py:80
  521.5 11.7 %cholesky.694 = f32[128,128]{1,0:T(8,128)S(1)} custom-call(f32[128,128]{1,0:T(8,128)S(1)} %cholesky.895), custom_call_target="Cholesky" | custom-call | tf_op jit(solution)/shard_map/jit(cholesky)/cholesky | solution.py:80
  562.2 11.9 %cholesky.656 = f32[128,128]{1,0:T(8,128)S(1)} custom-call(f32[128,128]{1,0:T(8,128)S(1)} %cholesky.892), custom_call_target="Cholesky" | custom-call | tf_op jit(solution)/shard_map/jit(cholesky)/cholesky | solution.py:80
  603.1 11.7 %cholesky.618 = f32[128,128]{1,0:T(8,128)S(1)} custom-call(f32[128,128]{1,0:T(8,128)S(1)} %cholesky.889), custom_call_target="Cholesky" | custom-call | tf_op jit(solution)/shard_map/jit(cholesky)/cholesky | solution.py:80
  644.2 11.7 %cholesky.580 = f32[128,128]{1,0:T(8,128)S(1)} custom-call(f32[128,128]{1,0:T(8,128)S(1)} %cholesky.886), custom_call_target="Cholesky" | custom-call | tf_op jit(solution)/shard_map/jit(cholesky)/cholesky | solution.py:80
  685.1 11.7 %cholesky.542 = f32[128,128]{1,0:T(8,128)S(1)} custom-call(f32[128,128]{1,0:T(8,128)S(1)} %cholesky.883), custom_call_target="Cholesky" | custom-call | tf_op jit(solution)/shard_map/jit(cholesky)/cholesky | solution.py:80
  726.6 20.5 %custom-call.32 = f32[2,128,128]{1,2,0:T(8,128)S(1)} custom-call(f32[2,128,128]{2,1,0:T(8,128)} %pad_maximum_fusion.10), custom_call_target="InvertDiagBlocksLowerTriangular" | custom-call | tf_op jit(solution)/shard_map/jit(_cho_solve)/triangular_solve | solution.py:97
  774.6 20.5 %custom-call.50 = f32[2,128,128]{1,2,0:T(8,128)S(1)} custom-call(f32[2,128,128]{2,1,0:T(8,128)} %pad_maximum_fusion.19), custom_call_target="InvertDiagBlocksLowerTriangular" | custom-call | tf_op jit(solution)/shard_map/jit(_cho_solve)/triangular_solve | solution.py:97
  795.1 20.3 %custom-call.36 = f32[2,128,128]{1,2,0:T(8,128)} custom-call(f32[2,128,128]{2,1,0:T(8,128)S(1)} %pad_maximum_fusion.12), custom_call_target="InvertDiagBlocksLowerTriangular" | custom-call | tf_op jit(solution)/shard_map/jit(_cho_solve)/triangular_solve | solution.py:97
  815.4 21.1 %custom-call.38 = f32[2,128,128]{1,2,0:T(8,128)} custom-call(f32[2,128,128]{2,1,0:T(8,128)} %pad_maximum_fusion.13), custom_call_target="InvertDiagBlocksLowerTriangular" | custom-call | tf_op jit(solution)/shard_map/jit(_cho_solve)/triangular_solve | solution.py:97
  836.5 21.1 %custom-call.40 = f32[2,128,128]{1,2,0:T(8,128)} custom-call(f32[2,128,128]{2,1,0:T(8,128)} %pad_maximum_fusion.14), custom_call_target="InvertDiagBlocksLowerTriangular" | custom-call | tf_op jit(solution)/shard_map/jit(_cho_solve)/triangular_solve | solution.py:97
  857.5 21.1 %custom-call.42 = f32[2,128,128]{1,2,0:T(8,128)} custom-call(f32[2,128,128]{2,1,0:T(8,128)} %pad_maximum_fusion.15), custom_call_target="InvertDiagBlocksLowerTriangular" | custom-call | tf_op jit(solution)/shard_map/jit(_cho_solve)/triangular_solve | solution.py:97
  878.6 20.4 %custom-call.44 = f32[2,128,128]{1,2,0:T(8,128)} custom-call(f32[2,128,128]{2,1,0:T(8,128)S(1)} %pad_maximum_fusion.16), custom_call_target="InvertDiagBlocksLowerTriangular" | custom-call | tf_op jit(solution)/shard_map/jit(_cho_solve)/triangular_solve | solution.py:97
  899.1 20.5 %custom-call.46 = f32[2,128,128]{1,2,0:T(8,128)S(1)} custom-call(f32[2,128,128]{2,1,0:T(8,128)} %pad_maximum_fusion.17), custom_call_target="InvertDiagBlocksLowerTriangular" | custom-call | tf_op jit(solution)/shard_map/jit(_cho_solve)/triangular_solve | solution.py:97
  919.6 20.5 %custom-call.48 = f32[2,128,128]{1,2,0:T(8,128)S(1)} custom-call(f32[2,128,128]{2,1,0:T(8,128)} %pad_maximum_fusion.18), custom_call_target="InvertDiagBlocksLowerTriangular" | custom-call | tf_op jit(solution)/shard_map/jit(_cho_solve)/triangular_solve | solution.py:97
  940.0 21.1 %custom-call.34 = f32[2,128,128]{1,2,0:T(8,128)} custom-call(f32[2,128,128]{2,1,0:T(8,128)} %pad_maximum_fusion.11), custom_call_target="InvertDiagBlocksLowerTriangular" | custom-call | tf_op jit(solution)/shard_map/jit(_cho_solve)/triangular_solve | solution.py:97
  (625 shorter events, 665.2 us)
Async XLA Ops:
  9.2 126.5 %copy-start.55 = (f32[1,2048]{1,0:T(1,128)}, f32[1,2048]{1,0:T(1,128)S(1)}, u32[]{:S(2)}) copy-start(f32[1,2048]{1,0:T(1,128)S(1)} %get-tuple-element.144) | copy-start | bytes 24580
  9.2 129.3 %copy-start.57 = (f32[1,2048]{1,0:T(1,128)}, f32[1,2048]{1,0:T(1,128)S(1)}, u32[]{:S(2)}) copy-start(f32[1,2048]{1,0:T(1,128)S(1)} %get-tuple-element.143) | copy-start | bytes 24580
  9.2 132.0 %copy-start.59 = (f32[1,2048]{1,0:T(1,128)}, f32[1,2048]{1,0:T(1,128)S(1)}, u32[]{:S(2)}) copy-start(f32[1,2048]{1,0:T(1,128)S(1)} %get-tuple-element.142) | copy-start | bytes 24580
  9.3 134.7 %copy-start.61 = (f32[1,2048]{1,0:T(1,128)}, f32[1,2048]{1,0:T(1,128)S(1)}, u32[]{:S(2)}) copy-start(f32[1,2048]{1,0:T(1,128)S(1)} %get-tuple-element.141) | copy-start | bytes 24580
  9.3 137.6 %copy-start.63 = (f32[1,2048]{1,0:T(1,128)}, f32[1,2048]{1,0:T(1,128)S(1)}, u32[]{:S(2)}) copy-start(f32[1,2048]{1,0:T(1,128)S(1)} %get-tuple-element.140) | copy-start | bytes 24580
  9.3 140.3 %copy-start.65 = (f32[1,2048]{1,0:T(1,128)}, f32[1,2048]{1,0:T(1,128)S(1)}, u32[]{:S(2)}) copy-start(f32[1,2048]{1,0:T(1,128)S(1)} %get-tuple-element.139) | copy-start | bytes 24580
  9.3 143.0 %copy-start.67 = (f32[1,2048]{1,0:T(1,128)}, f32[1,2048]{1,0:T(1,128)S(1)}, u32[]{:S(2)}) copy-start(f32[1,2048]{1,0:T(1,128)S(1)} %get-tuple-element.138) | copy-start | bytes 24580
  9.3 145.7 %copy-start.70 = (f32[1,2048]{1,0:T(1,128)}, f32[1,2048]{1,0:T(1,128)S(1)}, u32[]{:S(2)}) copy-start(f32[1,2048]{1,0:T(1,128)S(1)} %get-tuple-element.137) | copy-start | bytes 24580
  9.3 148.4 %copy-start.74 = (f32[1,2048]{1,0:T(1,128)}, f32[1,2048]{1,0:T(1,128)S(1)}, u32[]{:S(2)}) copy-start(f32[1,2048]{1,0:T(1,128)S(1)} %get-tuple-element.146) | copy-start | bytes 24580
  62.9 176.2 %all-to-all-start = ((f32[16,1,231]{2,1,0:T(1,128)}), f32[16,1,231]{2,1,0:T(1,128)S(1)}, u32[]{:S(2)}, u32[]{:S(2)}) async-start(f32[16,1,231]{2,1,0:T(1,128)} %broadcast_in_dim.208), calls=%async_computation | async-start | bytes 32768 | tf_op jit(solution)/shard_map/all_to_all | solution.py:23
  66.7 158.9 %all-reduce.8.cloned.1.call-start = ((), (), s32[]{:S(2)}) async-start(), calls=%async_computation.10 | async-start | bytes 4751360 | tf_op jit(solution)/shard_map/psum | solution.py:78
  160.5 130.9 %all-reduce.10.cloned.1.call-start = ((), (), s32[]{:S(2)}) async-start(), calls=%async_computation.11 | async-start | bytes 4751360 | tf_op jit(solution)/shard_map/psum | solution.py:78
  755.0 206.1 %all-to-all-start.1 = ((f32[16,1,231]{2,1,0:T(1,128)}), f32[16,1,231]{2,1,0:T(1,128)S(1)}, u32[]{:S(2)}, u32[]{:S(2)}) async-start(f32[16,1,231]{2,1,0:T(1,128)} %broadcast_in_dim.211), calls=%async_computation.1 | async-start | bytes 32768 | tf_op jit(solution)/shard_map/all_to_all | solution.py:23
  768.0 201.0 %copy-start.80 = (f32[2048]{0:T(1024)S(1)}, f32[2048]{0:T(1024)}, u32[]{:S(2)}) copy-start(f32[2048]{0:T(1024)} %reduce_sum.221) | copy-start | bytes 24580
  768.0 201.0 %copy-start.97 = (f32[1,2048]{1,0:T(1,128)S(1)}, f32[1,2048]{1,0:T(1,128)}, u32[]{:S(2)}) copy-start(f32[1,2048]{1,0:T(1,128)} %get-tuple-element.132) | copy-start | bytes 24580
  768.0 201.8 %copy-start.68 = (f32[1,2048]{1,0:T(1,128)S(1)}, f32[1,2048]{1,0:T(1,128)}, u32[]{:S(2)}) copy-start(f32[1,2048]{1,0:T(1,128)} %copy-done.67) | copy-start | bytes 24580
  973.6 15.1 %all-to-all-start.2 = ((f32[16,1,231]{2,1,0:T(1,128)}), f32[16,1,231]{2,1,0:T(1,128)S(1)}, u32[]{:S(2)}, u32[]{:S(2)}) async-start(f32[16,1,231]{2,1,0:T(1,128)} %broadcast_in_dim.214), calls=%async_computation.2 | async-start | bytes 32768 | tf_op jit(solution)/shard_map/all_to_all | solution.py:23
  997.0 11.0 all-to-all-start.3
  1016.3 11.0 all-to-all-start.4
  1035.6 11.4 all-to-all-start.5
  1055.3 11.0 all-to-all-start.6
  1076.3 11.0 all-to-all-start.7
  1097.2 11.2 all-to-all-start.8
  1118.3 11.0 all-to-all-start.9
  (97 other events, 1529.8 us)
Sparse Core Ops, SparseCore 0:
  160.6 64.9 all-reduce.7
  228.0 63.3 all-reduce.9
